TPU v7x, 32 devices: a whole 2x2x4 slice. The times are simulated.
32 devices in a mesh: rep: 4 (over z), ep: 8 (over y, x, core).
Axes of the slice: x: 2, y: 2, z: 4, core: 2. Of those that a mesh axis runs over, the one named last changes fastest.
Arguments:
- tokens: bfloat16 [32, 256, 2048], P('rep', 'ep'), may hold values from -6 to 6
- cotangent: bfloat16 [32, 256, 2048], P('rep', 'ep'), may hold values from -6 to 6
- gate_weights: bfloat16 [32, 256, 8], P('rep', 'ep'), may hold values from 0.049804688 to 0.25
- expert_ids: int32 [32, 256, 8], P('rep', 'ep'), may hold values from 0 to 15, all different within a row; in each aligned block of 256 rows (0 to 255, 256 to 511, ..., all dimensions but the last counted through in order) at most 144 rows name the same one
- seq_lengths: int32 [32], P(('rep', 'ep')), may hold values from 1 to 256, 5120 in all
- query_weight: bfloat16 [2048, 2048], P('ep'), may hold values from -0.125 to 0.125
- key_weight: bfloat16 [2048, 2048], P('ep'), may hold values from -0.125 to 0.125
- value_weight: bfloat16 [2048, 2048], P('ep'), may hold values from -0.125 to 0.125
- output_weight: bfloat16 [2048, 2048], P('ep'), may hold values from -0.75 to 0.75
- attn_gain: bfloat16 [2048], P('ep'), may hold values from 0.25 to 1.75
- ffn_gain: bfloat16 [2048], P('ep'), may hold values from 0.25 to 1.75
- query_gain: bfloat16 [128], P('ep'), may hold values from 0.25 to 1.75
- key_gain: bfloat16 [128], P('ep'), may hold values from 0.25 to 1.75
- expert_in: bfloat16 [16, 2048, 2048], P('ep'), may hold values from -0.125 to 0.125
- expert_out: bfloat16 [16, 1024, 2048], P('ep'), may hold values from -0.5 to 0.5
Outputs:
- result: bfloat16 [32, 256, 2048], P('rep', 'ep')
- token_grad: bfloat16 [32, 256, 2048], P('rep', 'ep')
- query_weight_grad: float32 [2048, 2048], P('ep')
- key_weight_grad: float32 [2048, 2048], P('ep')
- value_weight_grad: float32 [2048, 2048], P('ep')
- output_weight_grad: float32 [2048, 2048], P('ep')
- attn_gain_grad: float32 [2048], P('ep')
- ffn_gain_grad: float32 [2048], P('ep')
- query_gain_grad: float32 [128], P('ep')
- key_gain_grad: float32 [128], P('ep')
- expert_in_grad: float32 [16, 2048, 2048], P('ep', 'rep')
- expert_out_grad: float32 [16, 1024, 2048], P('ep', 'rep')
Inputs may be any that keep to these rules, and one draw needn't show every extreme that they name: `expert_ids`: each token names 8 different experts; within the 256 token slots of one sequence no expert is named more than 144 times, and some expert of some sequence is named exactly 144 times. `seq_lengths`: some sequence is full, with exactly 256 live tokens; live tokens come first in a sequence.
All inputs are finite; a program needn't handle non-finite values. No bound on the sum of `seq_lengths` on one device may be relied on, other than what follows from the above.
Results may differ from a plain program's by a relative error of at most 0.028.
Values may be sent and summed in bfloat16 or wider, within the bound.
A program may use at most 320 MiB of HBM per device.

v0:
```python
import jax
import jax.numpy as jnp
from jax import lax
from jax.sharding import PartitionSpec as P

HEADS = 16
HEAD_DIM = 128
epsilon = 1e-06
rope_base = 50000.0


def rms_norm(values, gain_vector):
    return (
        values
        * lax.rsqrt(jnp.mean(values * values, axis=-1, keepdims=True) + epsilon)
        * gain_vector
    )


def rotary_tables(length, head_width):
    half_width = head_width // 2
    frequency = rope_base ** (-(jnp.arange(half_width, dtype=jnp.float32) * (2.0 / head_width)))
    angles = jnp.arange(length, dtype=jnp.float32)[:, None] * frequency[None, :]
    angles = jnp.concatenate([angles, angles], axis=-1)
    return (jnp.cos(angles)[:, None, :], jnp.sin(angles)[:, None, :])


def rotate(values, cos_table, sin_table):
    half_width = values.shape[-1] // 2
    turned = jnp.concatenate([-values[..., half_width:], values[..., :half_width]], axis=-1)
    return values * cos_table + turned * sin_table


def slot_index(expert_ids, experts, capacity):
    flat_ids = expert_ids.reshape(-1)
    choose = (flat_ids[:, None] == jnp.arange(experts, dtype=jnp.int32)[None, :]).astype(jnp.int32)
    before = jnp.cumsum(choose, axis=0) - choose
    ranking = jnp.sum(before * choose, axis=1)
    return flat_ids * capacity + ranking


def contract(left_side, right_side, left_dim, right_dim):
    return lax.dot_general(
        left_side,
        right_side,
        (((left_dim,), (right_dim,)), ((), ())),
        preferred_element_type=jnp.float32,
    )


def masked_scores(query_low, key_low, living, score_scale):
    raw_scores = (
        jnp.einsum("qhd,khd->hqk", query_low, key_low, preferred_element_type=jnp.float32)
        * score_scale
    )
    return jnp.where(living[None, None, :] > 0.5, raw_scores, -1000000000.0)


def shards(
    tokens,
    cotangent,
    gate_weights,
    expert_ids,
    seq_lengths,
    query_weight,
    key_weight,
    value_weight,
    output_weight,
    attn_gain,
    ffn_gain,
    query_gain,
    key_gain,
    expert_in,
    expert_out,
):
    ep_count = lax.axis_size("ep")
    dealt_arrays = (
        lax.all_to_all(tokens, "ep", split_axis=0, concat_axis=1, tiled=True),
        lax.all_to_all(cotangent, "ep", split_axis=0, concat_axis=1, tiled=True),
        lax.all_to_all(gate_weights, "ep", split_axis=0, concat_axis=1, tiled=True),
    )
    seq_tokens = dealt_arrays[0][0]
    seq_cot = dealt_arrays[1][0]
    seq_gates = dealt_arrays[2][0]
    seq_ids = lax.all_to_all(expert_ids, "ep", split_axis=0, concat_axis=1, tiled=True)[0]
    length = seq_tokens.shape[0]
    model_width = seq_tokens.shape[1]
    top_count = seq_gates.shape[1]
    local_experts = expert_in.shape[0]
    hidden_size = expert_out.shape[1]
    experts = local_experts * ep_count
    capacity = length * top_count * 9 // (8 * experts)
    score_scale = HEAD_DIM ** (-0.5)
    gathered_weights = (
        lax.all_gather(query_weight, "ep", axis=0, tiled=True),
        lax.all_gather(key_weight, "ep", axis=0, tiled=True),
        lax.all_gather(value_weight, "ep", axis=0, tiled=True),
        lax.all_gather(output_weight, "ep", axis=0, tiled=True),
        lax.all_gather(attn_gain, "ep", axis=0, tiled=True),
        lax.all_gather(ffn_gain, "ep", axis=0, tiled=True),
        lax.all_gather(query_gain, "ep", axis=0, tiled=True),
        lax.all_gather(key_gain, "ep", axis=0, tiled=True),
    )
    w_query = gathered_weights[0]
    w_key = gathered_weights[1]
    w_value = gathered_weights[2]
    w_output = gathered_weights[3]
    gain_attn = gathered_weights[4].astype(jnp.float32)
    gain_ffn = gathered_weights[5].astype(jnp.float32)
    gain_query = gathered_weights[6].astype(jnp.float32)
    gain_key = gathered_weights[7].astype(jnp.float32)
    positions = jnp.arange(length, dtype=jnp.int32)
    living = (positions < seq_lengths[0]).astype(jnp.float32)
    combine_weight = seq_gates.astype(jnp.float32) * living[:, None]
    destination = slot_index(seq_ids, experts, capacity)
    pair_count = length * top_count
    token_of_slot = (
        jnp.zeros((experts * capacity,), jnp.int32)
        .at[destination]
        .set(jnp.arange(pair_count, dtype=jnp.int32) // top_count)
    )
    slot_weight = (
        jnp.zeros((experts * capacity,), jnp.float32)
        .at[destination]
        .set(combine_weight.reshape(-1))
    )
    slot_filled = (
        jnp.zeros((experts * capacity,), jnp.bfloat16)
        .at[destination]
        .set(jnp.ones((pair_count,), jnp.bfloat16))
    )
    cos_table, sin_table = rotary_tables(length, HEAD_DIM)

    def head_piece(inputs_pre, gain_vector):
        return rotate(rms_norm(inputs_pre, gain_vector), cos_table, sin_table)

    residual_in = seq_tokens.astype(jnp.float32)
    normed = rms_norm(residual_in, gain_attn).astype(jnp.bfloat16)
    query_pre = jnp.dot(normed, w_query, preferred_element_type=jnp.float32).reshape(
        length, HEADS, HEAD_DIM
    )
    key_pre = jnp.dot(normed, w_key, preferred_element_type=jnp.float32).reshape(
        length, HEADS, HEAD_DIM
    )
    value_low = (
        jnp.dot(normed, w_value, preferred_element_type=jnp.float32)
        .astype(jnp.bfloat16)
        .reshape(length, HEADS, HEAD_DIM)
    )
    query_rot, query_pull = jax.vjp(head_piece, query_pre, gain_query)
    key_rot, key_pull = jax.vjp(head_piece, key_pre, gain_key)
    query_low = query_rot.astype(jnp.bfloat16)
    key_low = key_rot.astype(jnp.bfloat16)
    scores = masked_scores(query_low, key_low, living, score_scale)
    log_total = jax.nn.logsumexp(scores, axis=-1, keepdims=True)
    attention_low = jnp.exp(scores - log_total).astype(jnp.bfloat16)
    context = jnp.einsum(
        "hqk,khd->qhd", attention_low, value_low, preferred_element_type=jnp.float32
    )
    context = context.astype(jnp.bfloat16).reshape(length, HEADS * HEAD_DIM)
    attended = jnp.dot(context, w_output, preferred_element_type=jnp.float32) * living[:, None]
    middle = residual_in + attended
    mixed_in = rms_norm(middle, gain_ffn).astype(jnp.bfloat16)
    outgoing = (mixed_in[token_of_slot] * slot_filled[:, None]).reshape(
        ep_count, local_experts, capacity, model_width
    )
    arrived = lax.all_to_all(outgoing, "ep", split_axis=0, concat_axis=2, tiled=True)[0]
    gate_up = jnp.einsum("erd,edf->erf", arrived, expert_in, preferred_element_type=jnp.float32)

    def swiglu(paired):
        return jax.nn.silu(paired[..., :hidden_size]) * paired[..., hidden_size:]

    activated, swiglu_pull = jax.vjp(swiglu, gate_up)
    activated_low = activated.astype(jnp.bfloat16)
    produced = jnp.einsum(
        "erf,efd->erd", activated_low, expert_out, preferred_element_type=jnp.float32
    ).astype(jnp.bfloat16)
    returned = lax.all_to_all(
        produced[None], "ep", split_axis=2, concat_axis=0, tiled=True
    ).reshape(experts * capacity, model_width)
    gathered = returned[destination].reshape(length, top_count, model_width).astype(jnp.float32)
    outcome = middle + jnp.sum(combine_weight[:, :, None] * gathered, axis=1)
    upstream = seq_cot.astype(jnp.float32)
    outgoing_grad = (upstream[token_of_slot] * slot_weight[:, None]).astype(jnp.bfloat16)
    outgoing_grad = outgoing_grad.reshape(ep_count, local_experts, capacity, model_width)
    arrived_grad = lax.all_to_all(outgoing_grad, "ep", split_axis=0, concat_axis=2, tiled=True)[0]
    activated_grad = jnp.einsum(
        "erd,efd->erf", arrived_grad, expert_out, preferred_element_type=jnp.float32
    )
    gate_up_grad = swiglu_pull(activated_grad)[0].astype(jnp.bfloat16)
    out_local_grad = jnp.einsum(
        "erf,erd->efd", activated_low, arrived_grad, preferred_element_type=jnp.float32
    )
    in_local_grad = jnp.einsum(
        "erd,erf->edf", arrived, gate_up_grad, preferred_element_type=jnp.float32
    )
    arrived_back = jnp.einsum(
        "erf,edf->erd", gate_up_grad, expert_in, preferred_element_type=jnp.float32
    ).astype(jnp.bfloat16)
    expert_sums = (
        lax.psum_scatter(
            in_local_grad.astype(jnp.bfloat16), "rep", scatter_dimension=1, tiled=True
        ).astype(jnp.float32),
        lax.psum_scatter(
            out_local_grad.astype(jnp.bfloat16), "rep", scatter_dimension=1, tiled=True
        ).astype(jnp.float32),
    )
    returned_grad = lax.all_to_all(
        arrived_back[None], "ep", split_axis=2, concat_axis=0, tiled=True
    ).reshape(experts * capacity, model_width)
    mixed_grad = jnp.sum(
        returned_grad[destination].reshape(length, top_count, model_width).astype(jnp.float32),
        axis=1,
    )
    ffn_values, ffn_pull = jax.vjp(rms_norm, middle, gain_ffn)
    middle_part, ffn_gain_grad = ffn_pull(mixed_grad)
    middle_grad = upstream + middle_part
    attended_grad = (middle_grad * living[:, None]).astype(jnp.bfloat16)
    output_weight_grad = contract(context, attended_grad, 0, 0)
    context_grad = (
        contract(attended_grad, w_output, 1, 1)
        .astype(jnp.bfloat16)
        .reshape(length, HEADS, HEAD_DIM)
    )
    attention_again = jnp.exp(masked_scores(query_low, key_low, living, score_scale) - log_total)
    attention_again_low = attention_again.astype(jnp.bfloat16)
    value_grad = jnp.einsum(
        "hqk,qhd->khd", attention_again_low, context_grad, preferred_element_type=jnp.float32
    )
    value_grad = value_grad.astype(jnp.bfloat16).reshape(length, HEADS * HEAD_DIM)
    prob_grad = jnp.einsum(
        "qhd,khd->hqk", context_grad, value_low, preferred_element_type=jnp.float32
    )
    score_grad = attention_again * (
        prob_grad - jnp.sum(attention_again * prob_grad, axis=-1, keepdims=True)
    )
    score_grad = score_grad.astype(jnp.bfloat16)
    query_rot_grad = (
        jnp.einsum("hqk,khd->qhd", score_grad, key_low, preferred_element_type=jnp.float32)
        * score_scale
    )
    key_rot_grad = (
        jnp.einsum("hqk,qhd->khd", score_grad, query_low, preferred_element_type=jnp.float32)
        * score_scale
    )
    query_grad, query_gain_grad = query_pull(query_rot_grad)
    key_grad, key_gain_grad = key_pull(key_rot_grad)
    query_grad = query_grad.astype(jnp.bfloat16).reshape(length, HEADS * HEAD_DIM)
    key_grad = key_grad.astype(jnp.bfloat16).reshape(length, HEADS * HEAD_DIM)
    normed_grad = (
        contract(query_grad, w_query, 1, 1)
        + contract(key_grad, w_key, 1, 1)
        + contract(value_grad, w_value, 1, 1)
    )
    query_weight_grad = contract(normed, query_grad, 0, 0)
    key_weight_grad = contract(normed, key_grad, 0, 0)
    value_weight_grad = contract(normed, value_grad, 0, 0)
    attn_values, attn_pull = jax.vjp(rms_norm, residual_in, gain_attn)
    input_part, attn_gain_grad = attn_pull(normed_grad)
    input_grad = (middle_grad + input_part).astype(jnp.bfloat16)
    moved_back = (
        lax.all_to_all(
            outcome.astype(jnp.bfloat16)[None], "ep", split_axis=1, concat_axis=0, tiled=True
        ),
        lax.all_to_all(input_grad[None], "ep", split_axis=1, concat_axis=0, tiled=True),
    )
    shares = (
        lax.psum_scatter(
            query_weight_grad.astype(jnp.bfloat16), "ep", scatter_dimension=0, tiled=True
        ).astype(jnp.float32),
        lax.psum_scatter(
            key_weight_grad.astype(jnp.bfloat16), "ep", scatter_dimension=0, tiled=True
        ).astype(jnp.float32),
        lax.psum_scatter(
            value_weight_grad.astype(jnp.bfloat16), "ep", scatter_dimension=0, tiled=True
        ).astype(jnp.float32),
        lax.psum_scatter(
            output_weight_grad.astype(jnp.bfloat16), "ep", scatter_dimension=0, tiled=True
        ).astype(jnp.float32),
        lax.psum_scatter(
            attn_gain_grad.astype(jnp.bfloat16), "ep", scatter_dimension=0, tiled=True
        ).astype(jnp.float32),
        lax.psum_scatter(
            ffn_gain_grad.astype(jnp.bfloat16), "ep", scatter_dimension=0, tiled=True
        ).astype(jnp.float32),
        lax.psum_scatter(
            query_gain_grad.astype(jnp.bfloat16), "ep", scatter_dimension=0, tiled=True
        ).astype(jnp.float32),
        lax.psum_scatter(
            key_gain_grad.astype(jnp.bfloat16), "ep", scatter_dimension=0, tiled=True
        ).astype(jnp.float32),
    )
    shares = (
        lax.psum(shares[0].astype(jnp.bfloat16), "rep").astype(jnp.float32),
        lax.psum(shares[1].astype(jnp.bfloat16), "rep").astype(jnp.float32),
        lax.psum(shares[2].astype(jnp.bfloat16), "rep").astype(jnp.float32),
        lax.psum(shares[3].astype(jnp.bfloat16), "rep").astype(jnp.float32),
        lax.psum(shares[4].astype(jnp.bfloat16), "rep").astype(jnp.float32),
        lax.psum(shares[5].astype(jnp.bfloat16), "rep").astype(jnp.float32),
        lax.psum(shares[6].astype(jnp.bfloat16), "rep").astype(jnp.float32),
        lax.psum(shares[7].astype(jnp.bfloat16), "rep").astype(jnp.float32),
    )
    return (
        moved_back[0],
        moved_back[1],
        shares[0],
        shares[1],
        shares[2],
        shares[3],
        shares[4],
        shares[5],
        shares[6],
        shares[7],
        expert_sums[0],
        expert_sums[1],
    )


def solution(mesh):
    return jax.shard_map(
        shards,
        mesh=mesh,
        in_specs=(
            P("rep", "ep", None),
            P("rep", "ep", None),
            P("rep", "ep", None),
            P("rep", "ep", None),
            P(("rep", "ep")),
            P("ep", None),
            P("ep", None),
            P("ep", None),
            P("ep", None),
            P("ep"),
            P("ep"),
            P("ep"),
            P("ep"),
            P("ep", None, None),
            P("ep", None, None),
        ),
        out_specs=(
            P("rep", "ep", None),
            P("rep", "ep", None),
            P("ep", None),
            P("ep", None),
            P("ep", None),
            P("ep", None),
            P("ep"),
            P("ep"),
            P("ep"),
            P("ep"),
            P("ep", "rep", None),
            P("ep", "rep", None),
        ),
        check_vma=False,
    )
```

profile of v0, /device:TPU:0, one launch (start us, length us, event | category | flops | bytes accessed | tf_op | source)
XLA Modules:
  0.0 1802.4 jit_solution(4447141272363571093)
XLA Ops:
  10.7 5.2 all-to-all-start.1
  24.0 9.7 all-gather
  35.4 13.8 all-reduce.13
  49.2 9.2 all-gather.1
  64.2 4.5 reduce-window.6
  69.8 8.1 all-to-all-done
  82.2 8.1 scatter_custom_fusion
  90.3 14.6 scatter_custom_fusion.1
  105.0 8.1 scatter_custom_fusion.2
  115.5 11.5 gather_fusion.2
  127.0 10.1 multiply_convert_fusion
  137.1 5.1 all-to-all-start.7
  142.9 11.9 copy.101
  154.8 12.5 copy.102
  167.3 6.0 multiply_reduce_fusion.9
  183.2 71.8 %all-gather.7.cloned.1.call-done = bf16[2048,2048]{1,0:T(8,128)(2,1)} async-done(((bf16[256,2048]{1,0:T(8,128)(2,1)}), bf16[2048,2048]{1,0:T(8,128)(2,1)}) %all-gather.7.cloned.1.call-update) | async-done | bytes 8388624 | tf_op jit(solution)/shard_map/all_gather | solution.py:97
  255.0 5.9 fusion.30
  263.1 66.4 %all-gather.13.cloned.1.call-done = bf16[2048,2048]{1,0:T(8,128)(2,1)} async-done(((bf16[256,2048]{1,0:T(8,128)(2,1)}), bf16[2048,2048]{1,0:T(8,128)(2,1)}) %all-gather.13.cloned.1.call-update) | async-done | bytes 8388624 | tf_op jit(solution)/shard_map/all_gather | solution.py:98
  329.5 15.4 multiply_reduce_fusion.7
  346.5 9.8 gather_fusion
  356.3 8.0 broadcast_multiply_fusion
  364.3 5.1 all-to-all-start.3
  369.5 9.2 copy.118
  378.7 96.1 %all-to-all-done.3 = bf16[8,2,144,2048]{3,2,1,0:T(8,128)(2,1)} async-done(((bf16[8,2,144,2048]{3,2,1,0:T(8,128)(2,1)}), bf16[8,2,144,2048]{3,2,1,0:T(8,128)(2,1)}, u32[]{:S(2)}, u32[]{:S(2)}) %all-to-all-start.3) | async-done | bytes 9437216 | tf_op jit(solution)/shard_map/all_to_all | solution.py:167
  474.8 9.2 copy.112
  484.0 27.4 %fusion.66 = f32[2,1152,2048]{2,1,0:T(8,128)} fusion(bf16[2,1152,2048]{2,1,0:T(8,128)(2,1)} %bitcast.188, bf16[2,2048,2048]{2,1,0:T(8,128)(2,1)} %param.28), kind=kOutput, calls=%fused_computation.165 | convolution fusion | flops 19327352832 | bytes 45088768 | tf_op jit(solution)/shard_map/erd,edf->erf/dot_general | solution.py:168
  511.4 27.5 %fusion.31 = (f32[2,1152,1024]{2,1,0:T(8,128)}, f32[2,1152,1024]{2,1,0:T(8,128)}, bf16[2,1152,1024]{2,1,0:T(8,128)(2,1)}) fusion(f32[2,1152,2048]{2,1,0:T(8,128)} %fusion.66, bf16[2,1152,2048]{2,1,0:T(8,128)(2,1)} %bitcast.190, bf16[2,1024,2048]{2,1,0:T(8,128)(2,1)} %param.29), kind=kOutput, calls=%fused_computation.95 | convolution fusion | flops 9696706560 | bytes 60293120 | tf_op jit(solution)/shard_map/erd,efd->erf/dot_general | solution.py:187
  538.8 14.6 fusion.4
  553.5 27.9 %copy.113 = bf16[1,2,1152,2048]{3,1,0,2:T(2,128)(2,1)} copy(bf16[1,2,1152,2048]{3,2,1,0:T(8,128)(2,1)S(1)} %fusion.4) | data formatting | bytes 18874368 | tf_op jit(solution)/shard_map/broadcast_in_dim | solution.py:179
  581.4 5.1 all-to-all-start.4
  586.5 27.6 %fusion.5 = bf16[1,2,1152,2048]{3,2,1,0:T(8,128)(2,1)} fusion(bf16[2,2048,2048]{2,1,0:T(8,128)(2,1)} %param.28, f32[2,1152,1024]{2,1,0:T(8,128)} %get-tuple-element.37, f32[2,1152,1024]{2,1,0:T(8,128)} %get-tuple-element.36), kind=kOutput, calls=%fused_computation.22 | convolution fusion | flops 19341508608 | bytes 45088768 | tf_op jit(solution)/shard_map/erf,edf->erd/dot_general | solution.py:197
  614.1 18.2 %copy.119 = bf16[1,2,1152,2048]{3,1,0,2:T(2,128)(2,1)} copy(bf16[1,2,1152,2048]{3,2,1,0:T(8,128)(2,1)} %fusion.5) | data formatting | bytes 18874368 | tf_op jit(solution)/shard_map/broadcast_in_dim | solution.py:209
  632.3 59.5 %all-to-all-done.4 = bf16[1,2,1152,2048]{3,1,0,2:T(2,128)(2,1)} async-done(((bf16[1,2,1152,2048]{3,1,0,2:T(2,128)(2,1)}), bf16[1,2,1152,2048]{3,1,0,2:T(2,128)(2,1)}, u32[]{:S(2)}, u32[]{:S(2)}) %all-to-all-start.4) | async-done | bytes 9437216 | tf_op jit(solution)/shard_map/all_to_all | solution.py:178
  691.8 5.0 all-to-all-start.8
  697.3 11.7 copy.114
  709.0 93.1 %all-to-all-done.8 = bf16[1,2,1152,2048]{3,1,0,2:T(2,128)(2,1)} async-done(((bf16[1,2,1152,2048]{3,1,0,2:T(2,128)(2,1)}), bf16[1,2,1152,2048]{3,1,0,2:T(2,128)(2,1)}, u32[]{:S(2)}, u32[]{:S(2)}) %all-to-all-start.8) | async-done | bytes 9437216 | tf_op jit(solution)/shard_map/all_to_all | solution.py:208
  802.1 11.8 copy.120
  813.9 21.2 %gather_fusion.1 = bf16[2048,2048]{1,0:T(8,128)(2,1)} fusion(bf16[2304,2048]{1,0:T(8,128)(2,1)} %bitcast.178, s32[2048]{0:T(1024)S(1)} %broadcast_clamp_fusion), kind=kCustom, calls=%fused_computation.1 | custom fusion | bytes 16785408 | tf_op jit(solution)/shard_map/gather | solution.py:181
  835.1 21.4 %gather_fusion.3 = bf16[2048,2048]{1,0:T(8,128)(2,1)} fusion(bf16[2304,2048]{1,0:T(8,128)(2,1)} %bitcast.179, s32[2048]{0:T(1024)S(1)} %broadcast_clamp_fusion), kind=kCustom, calls=%fused_computation.3 | custom fusion | bytes 16785408 | tf_op jit(solution)/shard_map/gather | solution.py:212
  856.5 11.4 convert_reduce_fusion
  870.1 12.9 fusion
  888.5 5.8 convolution_convert_fusion.8
  899.6 5.7 convolution_convert_fusion.4
  906.9 7.7 convolution_convert_fusion.3
  916.5 4.4 multiply_reduce_fusion
  931.9 5.7 convolution_convert_fusion.5
  941.5 5.8 convolution_convert_fusion.6
  947.4 17.9 convolution_convert_fusion.7
  965.3 10.8 reduce-scatter.11.cloned.1.call-done
  976.2 74.9 %reduce-scatter.13.cloned.1.call-done = bf16[256,2048]{1,0:T(8,128)(2,1)} async-done(((bf16[2048,2048]{1,0:T(8,128)(2,1)}), bf16[256,2048]{1,0:T(8,128)(2,1)}) %reduce-scatter.13.cloned.1.call-update) | async-done | bytes 1048592 | tf_op jit(solution)/shard_map/reduce_scatter | solution.py:277
  1051.0 75.0 %reduce-scatter.9.cloned.1.call-done = bf16[256,2048]{1,0:T(8,128)(2,1)} async-done(((bf16[2048,2048]{1,0:T(8,128)(2,1)}), bf16[256,2048]{1,0:T(8,128)(2,1)}) %reduce-scatter.9.cloned.1.call-update) | async-done | bytes 1048592 | tf_op jit(solution)/shard_map/reduce_scatter | solution.py:271
  1126.0 75.6 %reduce-scatter.7.cloned.1.call-done = bf16[256,2048]{1,0:T(8,128)(2,1)} async-done(((bf16[2048,2048]{1,0:T(8,128)(2,1)}), bf16[256,2048]{1,0:T(8,128)(2,1)}) %reduce-scatter.7.cloned.1.call-update) | async-done | bytes 1048592 | tf_op jit(solution)/shard_map/reduce_scatter | solution.py:268
  1201.7 29.4 %convolution_convert_fusion = bf16[2,2048,2048]{2,1,0:T(8,128)(2,1)} fusion(bf16[2,1152,2048]{2,1,0:T(8,128)(2,1)} %bitcast.189, f32[2,1152,1024]{2,1,0:T(8,128)} %get-tuple-element.37, f32[2,1152,1024]{2,1,0:T(8,128)} %get-tuple-element.36), kind=kOutput, calls=%fused_computation.13 | convolution fusion | flops 19345178624 | bytes 45088768 | tf_op jit(solution)/shard_map/erd,erf->edf/dot_general | solution.py:194
  1232.3 5.9 fusion.68
  1238.2 6.0 convolution_add_fusion.1
  1249.9 8.0 reduce.8
  1266.4 6.8 reduce.7
  1274.8 5.4 all-to-all-done.9
  1285.0 21.1 %all-reduce.12 = (bf16[2048]{0:T(1024)(128)(2,1)S(1)}, bf16[2048]{0:T(1024)(128)(2,1)S(1)}, bf16[128]{0:T(256)(128)(2,1)S(1)}, bf16[128]{0:T(256)(128)(2,1)S(1)}) all-reduce(bf16[2048]{0:T(1024)(128)(2,1)S(1)} %get-tuple-element.18, bf16[2048]{0:T(1024)(128)(2,1)S(1)} %get-tuple-element.16, ...), channel_id=6, replica_groups=mesh['rep'=4,'ep'=8] {'ep'}, use_global_device_ids=true, to_apply=%region_28.29.clone | all-reduce | flops 4352 | bytes 17408
  1306.5 12.4 all-reduce.14
  1329.6 19.3 %reduce-scatter.17.cloned.1.call-done = bf16[2,256,2048]{2,1,0:T(8,128)(2,1)} async-done(((bf16[2,1024,2048]{2,1,0:T(8,128)(2,1)}), bf16[2,256,2048]{2,1,0:T(8,128)(2,1)}) %reduce-scatter.17.cloned.1.call-update) | async-done | bytes 2097168 | tf_op jit(solution)/shard_map/reduce_scatter | solution.py:204
  1353.0 153.9 %all-reduce.18.cloned.1.call-done = (bf16[256,2048]{1,0:T(8,128)(2,1)}, bf16[256,2048]{1,0:T(8,128)(2,1)}, bf16[256,2048]{1,0:T(8,128)(2,1)}, bf16[256,2048]{1,0:T(8,128)(2,1)}) async-done(((bf16[256,2048]{1,0:T(8,128)(2,1)}, bf16[256,2048]{1,0:T(8,128)(2,1)}, bf16[256,2048]{1,0:T(8,128)(2,1)}, bf16[256,2048]{1,0:T(8,128)(2,1)}), (bf16[256,2048]{1,0:T(8,128)(2,1)}, bf16[256,2048]{1,0:T(8,128)(2,1)}, ...) | async-done | bytes 4194320 | tf_op jit(solution)/shard_map/psum | solution.py:294
  1515.8 273.0 %reduce-scatter.15.cloned.1.call-done = bf16[2,512,2048]{2,1,0:T(8,128)(2,1)} async-done(((bf16[2,2048,2048]{2,1,0:T(8,128)(2,1)}), bf16[2,512,2048]{2,1,0:T(8,128)(2,1)}) %reduce-scatter.15.cloned.1.call-update) | async-done | bytes 4194320 | tf_op jit(solution)/shard_map/reduce_scatter | solution.py:201
  1788.8 6.7 convert_element_type.294
  (306 shorter events, 115.5 us)
Async XLA Ops:
  7.2 26.5 %copy-start.73 = (u32[32]{0:T(128)S(1)}, u32[32]{0:T(128)}, u32[]{:S(2)}) copy-start(u32[32]{0:T(128)} %constant.91) | copy-start | bytes 388
  7.2 10.7 copy-start.53
  7.2 16.7 copy-start.74
  7.2 27.7 %copy-start.75 = (bf16[16]{0:T(256)(128)(2,1)S(1)}, bf16[16]{0:T(256)(128)(2,1)}, u32[]{:S(2)}) copy-start(bf16[16]{0:T(256)(128)(2,1)} %param.26) | copy-start | bytes 100
  7.2 28.0 %copy-start.76 = (bf16[16]{0:T(256)(128)(2,1)S(1)}, bf16[16]{0:T(256)(128)(2,1)}, u32[]{:S(2)}) copy-start(bf16[16]{0:T(256)(128)(2,1)} %param.27) | copy-start | bytes 100
  7.2 42.0 %copy-start.77 = (bf16[256]{0:T(256)(128)(2,1)S(1)}, bf16[256]{0:T(256)(128)(2,1)}, u32[]{:S(2)}) copy-start(bf16[256]{0:T(256)(128)(2,1)} %param.25) | copy-start | bytes 1540
  7.3 135.6 %all-gather.9.cloned.1.call-start = ((), (), s32[]{:S(2)}) async-start(), calls=%async_computation.17 | async-start | bytes 9437184 | tf_op jit(solution)/shard_map/all_gather | solution.py:95
  8.0 146.8 %all-gather.11.cloned.1.call-start = ((), (), s32[]{:S(2)}) async-start(), calls=%async_computation.18 | async-start | bytes 9437184 | tf_op jit(solution)/shard_map/all_gather | solution.py:96
  8.7 246.3 %all-gather.7.cloned.1.call-start = ((), (), s32[]{:S(2)}) async-start(), calls=%async_computation.16 | async-start | bytes 9437184 | tf_op jit(solution)/shard_map/all_gather | solution.py:97
  9.5 320.0 %all-gather.13.cloned.1.call-start = ((), (), s32[]{:S(2)}) async-start(), calls=%async_computation.19 | async-start | bytes 9437184 | tf_op jit(solution)/shard_map/all_gather | solution.py:98
  10.7 9.8 all-to-all-start.1
  17.9 311.6 %copy-start.59 = (f32[256]{0:T(256)}, f32[256]{0:T(256)S(1)}, u32[]{:S(2)}) copy-start(f32[256]{0:T(256)S(1)} %compare_convert_fusion) | copy-start | bytes 3076
  20.6 38.4 %all-to-all-start.2 = ((s32[8,1,256]{2,1,0:T(1,128)}), s32[8,1,256]{2,1,0:T(1,128)S(1)}, u32[]{:S(2)}, u32[]{:S(2)}) async-start(s32[8,1,256]{2,1,0:T(1,128)} %reshape.509), calls=%async_computation.2 | async-start | bytes 16384 | tf_op jit(solution)/shard_map/all_to_all | solution.py:85
  23.9 237.0 %copy-start.67 = (pred[256]{0:T(512)(128)(4,1)}, pred[256]{0:T(512)(128)(4,1)S(1)}, u32[]{:S(2)}) copy-start(pred[256]{0:T(512)(128)(4,1)S(1)} %broadcast_compare_fusion) | copy-start | bytes 772
  33.6 108.9 %copy-start.45 = (f32[8,1,256]{2,1,0:T(1,128)}, f32[8,1,256]{2,1,0:T(1,128)S(1)}, u32[]{:S(2)}) copy-start(f32[8,1,256]{2,1,0:T(1,128)S(1)} %convert_element_type.303) | copy-start | bytes 24580
  49.2 127.7 %copy-start.69 = (f32[128]{0:T(128)}, f32[128]{0:T(128)S(1)}, u32[]{:S(2)}) copy-start(f32[128]{0:T(128)S(1)} %convert_element_type.242) | copy-start | bytes 1540
  49.2 127.6 %copy-start.71 = (f32[128]{0:T(128)}, f32[128]{0:T(128)S(1)}, u32[]{:S(2)}) copy-start(f32[128]{0:T(128)S(1)} %convert_element_type.244) | copy-start | bytes 1540
  58.5 286.5 %copy-start.47 = (f32[8,1,256]{2,1,0:T(1,128)}, f32[8,1,256]{2,1,0:T(1,128)S(1)}, u32[]{:S(2)}) copy-start(f32[8,1,256]{2,1,0:T(1,128)S(1)} %convert_element_type.304) | copy-start | bytes 24580
  58.8 5.3 copy-start.43
  59.0 18.9 %all-to-all-start = ((bf16[8,32,2048]{2,1,0:T(8,128)(2,1)}), bf16[8,32,2048]{2,1,0:T(8,128)(2,1)S(1)}, u32[]{:S(2)}, u32[]{:S(2)}) async-start(bf16[8,32,2048]{2,1,0:T(8,128)(2,1)} %param.15), calls=%async_computation | async-start | bytes 2097152 | tf_op jit(solution)/shard_map/all_to_all | solution.py:78
  77.9 251.6 %copy-start.3 = (bf16[8,32,2048]{2,1,0:T(8,128)(2,1)}, bf16[8,32,2048]{2,1,0:T(8,128)(2,1)S(1)}, u32[]{:S(2)}) copy-start(bf16[8,32,2048]{2,1,0:T(8,128)(2,1)S(1)} %all-to-all-done) | copy-start | bytes 3145732
  77.9 36.2 %all-to-all-start.6 = ((bf16[8,32,2048]{2,1,0:T(8,128)(2,1)}), bf16[8,32,2048]{2,1,0:T(8,128)(2,1)}, u32[]{:S(2)}, u32[]{:S(2)}) async-start(bf16[8,32,2048]{2,1,0:T(8,128)(2,1)} %param.16), calls=%async_computation.6 | async-start | bytes 2097152 | tf_op jit(solution)/shard_map/all_to_all | solution.py:79
  82.2 22.8 %copy-start.54 = (s32[2048,1]{0,1:T(1,128)}, s32[2048,1]{0,1:T(1,128)S(1)}, u32[]{:S(2)}) copy-start(s32[2048,1]{0,1:T(1,128)S(1)} %compare_select_fusion) | copy-start | bytes 24580
  114.1 28.4 %copy-start.61 = (f32[256]{0:T(256)}, f32[256]{0:T(256)S(1)}, u32[]{:S(2)}) copy-start(f32[256]{0:T(256)S(1)} %rsqrt.45) | copy-start | bytes 3076
  137.1 227.2 %all-to-all-start.7 = ((bf16[8,2,144,2048]{3,2,1,0:T(8,128)(2,1)}), bf16[8,2,144,2048]{3,2,1,0:T(8,128)(2,1)}, u32[]{:S(2)}, u32[]{:S(2)}) async-start(bf16[8,2,144,2048]{3,2,1,0:T(8,128)(2,1)} %multiply_convert_fusion), calls=%async_computation.7 | async-start | bytes 18874368 | tf_op jit(solution)/shard_map/all_to_all | solution.py:186
  142.5 31.3 %copy-start.7 = (bf16[8,32,2048]{2,1,0:T(8,128)(2,1)}, bf16[8,32,2048]{2,1,0:T(8,128)(2,1)S(1)}, u32[]{:S(2)}) copy-start(bf16[8,32,2048]{2,1,0:T(8,128)(2,1)S(1)} %fusion.28) | copy-start | bytes 3145732
  167.2 6.6 copy-start.20
  183.2 77.7 %copy-start.41 = (f32[16,256]{1,0:T(8,128)}, f32[16,256]{1,0:T(8,128)S(1)}, u32[]{:S(2)}) copy-start(f32[16,256]{1,0:T(8,128)S(1)} %log_add_fusion) | copy-start | bytes 49156
  255.0 6.9 copy-start.1
  263.1 81.9 %copy-start.21 = (bf16[16,128,256]{2,1,0:T(8,128)(2,1)}, bf16[16,128,256]{2,1,0:T(8,128)(2,1)S(1)}, u32[]{:S(2)}) copy-start(bf16[16,128,256]{2,1,0:T(8,128)(2,1)S(1)} %convolution_convert_fusion.11) | copy-start | bytes 3145732
  344.9 11.4 copy-start.63
  345.0 11.4 copy-start.56
  364.3 110.4 %all-to-all-start.3 = ((bf16[8,2,144,2048]{3,2,1,0:T(8,128)(2,1)}), bf16[8,2,144,2048]{3,2,1,0:T(8,128)(2,1)}, u32[]{:S(2)}, u32[]{:S(2)}) async-start(bf16[8,2,144,2048]{3,2,1,0:T(8,128)(2,1)} %broadcast_multiply_fusion), calls=%async_computation.3 | async-start | bytes 18874368 | tf_op jit(solution)/shard_map/all_to_all | solution.py:167
  581.4 110.4 %all-to-all-start.4 = ((bf16[1,2,1152,2048]{3,1,0,2:T(2,128)(2,1)}), bf16[1,2,1152,2048]{3,1,0,2:T(2,128)(2,1)}, u32[]{:S(2)}, u32[]{:S(2)}) async-start(bf16[1,2,1152,2048]{3,1,0,2:T(2,128)(2,1)} %copy.113), calls=%async_computation.4 | async-start | bytes 18874368 | tf_op jit(solution)/shard_map/all_to_all | solution.py:178
  632.3 64.7 %copy-start.44 = (bf16[8,8,32]{2,1,0:T(8,128)(2,1)S(1)}, bf16[8,8,32]{2,1,0:T(8,128)(2,1)}, u32[]{:S(2)}) copy-start(bf16[8,8,32]{2,1,0:T(8,128)(2,1)} %copy-done.43) | copy-start | bytes 12292
  632.3 64.8 %copy-start.60 = (f32[256]{0:T(256)S(1)}, f32[256]{0:T(256)}, u32[]{:S(2)}) copy-start(f32[256]{0:T(256)} %copy-done.59) | copy-start | bytes 3076
  632.3 65.0 %copy-start.55 = (s32[2048,1]{0,1:T(1,128)S(1)}, s32[2048,1]{0,1:T(1,128)}, u32[]{:S(2)}) copy-start(s32[2048,1]{0,1:T(1,128)} %copy-done.54) | copy-start | bytes 24580
  691.8 110.3 %all-to-all-start.8 = ((bf16[1,2,1152,2048]{3,1,0,2:T(2,128)(2,1)}), bf16[1,2,1152,2048]{3,1,0,2:T(2,128)(2,1)}, u32[]{:S(2)}, u32[]{:S(2)}) async-start(bf16[1,2,1152,2048]{3,1,0,2:T(2,128)(2,1)} %copy.119), calls=%async_computation.8 | async-start | bytes 18874368 | tf_op jit(solution)/shard_map/all_to_all | solution.py:208
  696.8 279.3 %reduce-scatter.11.cloned.1.call-start = ((), (), s32[]{:S(2)}) async-start(), calls=%async_computation.22 | async-start | bytes 9437184 | tf_op jit(solution)/shard_map/reduce_scatter | solution.py:274
  856.5 11.5 copy-start.6
  856.5 11.4 copy-start.48
  856.5 11.4 copy-start.57
  888.5 6.3 copy-start.42
  888.5 6.3 copy-start.68
  894.3 5.3 copy-start.8
  894.8 10.5 copy-start.23
  905.3 145.7 %reduce-scatter.13.cloned.1.call-start = ((), (), s32[]{:S(2)}) async-start(), calls=%async_computation.23 | async-start | bytes 9437184 | tf_op jit(solution)/shard_map/reduce_scatter | solution.py:277
  914.6 211.4 %reduce-scatter.9.cloned.1.call-start = ((), (), s32[]{:S(2)}) async-start(), calls=%async_computation.21 | async-start | bytes 9437184 | tf_op jit(solution)/shard_map/reduce_scatter | solution.py:271
  937.6 264.0 %reduce-scatter.7.cloned.1.call-start = ((), (), s32[]{:S(2)}) async-start(), calls=%async_computation.20 | async-start | bytes 9437184 | tf_op jit(solution)/shard_map/reduce_scatter | solution.py:268
  947.3 401.6 %reduce-scatter.17.cloned.1.call-start = ((), (), s32[]{:S(2)}) async-start(), calls=%async_computation.25 | async-start | bytes 10485760 | tf_op jit(solution)/shard_map/reduce_scatter | solution.py:204
  965.3 541.7 %all-reduce.18.cloned.1.call-start = ((), (), s32[]{:S(2)}) async-start(), calls=%async_computation.26 | async-start | bytes 8388608 | tf_op jit(solution)/shard_map/psum | solution.py:294
  1201.6 587.2 %reduce-scatter.15.cloned.1.call-start = ((), (), s32[]{:S(2)}) async-start(), calls=%async_computation.24 | async-start | bytes 20971520 | tf_op jit(solution)/shard_map/reduce_scatter | solution.py:201
  1232.3 5.9 copy-start.26
  1232.3 12.0 slice-start
  1238.2 6.1 copy-start.4
  1238.2 6.1 copy-start.32
  1238.2 6.1 copy-start.46
  1238.2 6.1 copy-start.62
  1238.2 6.1 slice-start.1
  1249.4 15.4 copy-start.22
  1260.5 19.6 %all-to-all-start.9 = ((bf16[8,2,32768]{2,1,0:T(2,128)(2,1)}), bf16[8,2,32768]{2,1,0:T(2,128)(2,1)}, u32[]{:S(2)}, u32[]{:S(2)}) async-start(bf16[8,2,32768]{2,1,0:T(2,128)(2,1)} %reshape.515), calls=%async_computation.9 | async-start | bytes 2097152 | tf_op jit(solution)/shard_map/all_to_all | solution.py:265
  1280.2 46.8 %all-to-all-start.5 = ((bf16[8,2,32768]{2,1,0:T(2,128)(2,1)}), bf16[8,2,32768]{2,1,0:T(2,128)(2,1)S(1)}, u32[]{:S(2)}, u32[]{:S(2)}) async-start(bf16[8,2,32768]{2,1,0:T(2,128)(2,1)} %reshape.513), calls=%async_computation.5 | async-start | bytes 2097152 | tf_op jit(solution)/shard_map/all_to_all | solution.py:262
  1506.9 5.7 copy-start.30
  1506.9 7.3 copy-start.29
  (37 other events, 71.9 us)
Sparse Core Ops, SparseCore 0:
  9.9 57.3 all-gather.8
  69.2 65.4 all-gather.10
  136.5 118.4 all-gather.6
  256.7 72.6 all-gather.12
  905.4 70.6 reduce-scatter.10
  979.5 71.5 reduce-scatter.12
  1054.5 71.5 reduce-scatter.8
  1130.1 71.4 reduce-scatter.6
  1204.0 144.8 reduce-scatter.16
  1351.3 155.5 all-reduce.17
  1509.3 279.4 reduce-scatter.14
where the time goes:
time: 1810 us; the launch traced here: 1800 us
  waiting for transfers between devices  1090 us (60%)
  local copies, waits for them, and re-layouts  247 us (14%)
  matrix products  231 us (13%)
  other arithmetic  106 us (6%)
  blocking collectives  66.2 us (4%)
  starting transfers between devices  45.7 us (3%)
  between operations  18.4 us (1%)
    reduce_scatter x1, waiting for transfers between devices, shards(): lax.psum_scatter(in_local_grad.astype(jnp.bfloat16), 'rep', scatter_dimen...  273 us
    psum x1, waiting for transfers between devices, shards(): lax.psum(shares[0].astype(jnp.bfloat16), 'rep').astype(jnp.float32)  154 us
    all_to_all x1, waiting for transfers between devices, shards(): lax.all_to_all(outgoing, 'ep', split_axis=0, concat_axis=2, tiled=True)[0]  96.1 us
    all_to_all x1, waiting for transfers between devices, shards(): lax.all_to_all(arrived_back[None], 'ep', split_axis=2, concat_axis=0, til...  93.1 us
    reduce_scatter x1, waiting for transfers between devices, shards(): lax.psum_scatter(query_weight_grad.astype(jnp.bfloat16), 'ep', scatter_di...  75.6 us
    reduce_scatter x1, waiting for transfers between devices, shards(): lax.psum_scatter(key_weight_grad.astype(jnp.bfloat16), 'ep', scatter_dime...  75 us
    reduce_scatter x1, waiting for transfers between devices, shards(): lax.psum_scatter(output_weight_grad.astype(jnp.bfloat16), 'ep', scatter_d...  74.9 us
    all_gather x1, waiting for transfers between devices, shards(): lax.all_gather(value_weight, 'ep', axis=0, tiled=True)  71.8 us
  transfers between devices with their start and end apart: 21, of which 15 were waited for; matrix products, arithmetic and copies ran while one was open for 20% of the time, Pallas kernels for 0%

commit v1 on v0

--- a/solution.py
+++ b/solution.py
@@ -7,6 +7,12 @@
 HEAD_DIM = 128
 epsilon = 1e-06
 rope_base = 50000.0
+
+
+def swap_blocks(array, axis, split, join):
+    pieces = jnp.split(array, lax.axis_size(axis), axis=split)
+    received = lax.all_to_all(jnp.stack(pieces), axis, 0, 0)
+    return jnp.concatenate(received, axis=join)
 
 
 def rms_norm(values, gain_vector):
@@ -164,7 +170,7 @@
     outgoing = (mixed_in[token_of_slot] * slot_filled[:, None]).reshape(
         ep_count, local_experts, capacity, model_width
     )
-    arrived = lax.all_to_all(outgoing, "ep", split_axis=0, concat_axis=2, tiled=True)[0]
+    arrived = swap_blocks(outgoing, "ep", 0, 2)[0]
     gate_up = jnp.einsum("erd,edf->erf", arrived, expert_in, preferred_element_type=jnp.float32)
 
     def swiglu(paired):

time: 1810 us -> 1830 us (1.011)
    unnamed x182 -> x189, local copies, waits for them, and re-layouts: 34 us -> 41.7 us
where the time goes in v1:
time: 1830 us; the launch traced here: 1820 us
  waiting for transfers between devices  1090 us (60%)
  local copies, waits for them, and re-layouts  261 us (14%)
  matrix products  232 us (13%)
  other arithmetic  106 us (6%)
  blocking collectives  66.2 us (4%)
  starting transfers between devices  45.6 us (2%)
  between operations  18.4 us (1%)
    reduce_scatter x1, waiting for transfers between devices, shards(): lax.psum_scatter(in_local_grad.astype(jnp.bfloat16), 'rep', scatter_dimen...  273 us
    psum x1, waiting for transfers between devices, shards(): lax.psum(shares[0].astype(jnp.bfloat16), 'rep').astype(jnp.float32)  154 us
    all_to_all x1, waiting for transfers between devices, swap_blocks(): received = lax.all_to_all(jnp.stack(pieces), axis, 0, 0)  96.1 us
    all_to_all x1, waiting for transfers between devices, shards(): lax.all_to_all(arrived_back[None], 'ep', split_axis=2, concat_axis=0, til...  93.1 us
    reduce_scatter x1, waiting for transfers between devices, shards(): lax.psum_scatter(query_weight_grad.astype(jnp.bfloat16), 'ep', scatter_di...  75.6 us
    reduce_scatter x1, waiting for transfers between devices, shards(): lax.psum_scatter(key_weight_grad.astype(jnp.bfloat16), 'ep', scatter_dime...  75 us
    reduce_scatter x1, waiting for transfers between devices, shards(): lax.psum_scatter(output_weight_grad.astype(jnp.bfloat16), 'ep', scatter_d...  74.9 us
    all_gather x1, waiting for transfers between devices, shards(): lax.all_gather(value_weight, 'ep', axis=0, tiled=True)  71 us
  transfers between devices with their start and end apart: 21, of which 15 were waited for; matrix products, arithmetic and copies ran while one was open for 20% of the time, Pallas kernels for 0%

profile of v1, /device:TPU:0, one launch (start us, length us, event | category | flops | bytes accessed | tf_op | source)
XLA Modules:
  0.0 1815.9 jit_solution(14201728191034140217)
XLA Ops:
  10.7 5.2 all-to-all-start.1
  24.0 9.7 all-gather
  35.4 13.8 all-reduce.13
  49.2 9.2 all-gather.1
  64.2 4.5 reduce-window.6
  69.8 8.1 all-to-all-done
  82.2 8.1 scatter_custom_fusion
  90.3 8.1 scatter_custom_fusion.2
  98.4 14.6 scatter_custom_fusion.1
  115.4 11.5 gather_fusion.2
  126.9 10.1 multiply_convert_fusion
  137.0 5.1 all-to-all-start.7
  142.8 12.7 copy.114
  155.5 12.5 copy.115
  168.0 6.0 multiply_reduce_fusion.9
  184.0 71.0 %all-gather.7.cloned.1.call-done = bf16[2048,2048]{1,0:T(8,128)(2,1)} async-done(((bf16[256,2048]{1,0:T(8,128)(2,1)}), bf16[2048,2048]{1,0:T(8,128)(2,1)}) %all-gather.7.cloned.1.call-update) | async-done | bytes 8388624 | tf_op jit(solution)/shard_map/all_gather | solution.py:103
  254.9 5.9 fusion.30
  263.0 66.4 %all-gather.13.cloned.1.call-done = bf16[2048,2048]{1,0:T(8,128)(2,1)} async-done(((bf16[256,2048]{1,0:T(8,128)(2,1)}), bf16[2048,2048]{1,0:T(8,128)(2,1)}) %all-gather.13.cloned.1.call-update) | async-done | bytes 8388624 | tf_op jit(solution)/shard_map/all_gather | solution.py:104
  329.4 16.2 multiply_reduce_fusion.7
  347.1 9.9 gather_fusion
  357.0 8.0 broadcast_multiply_fusion
  378.0 5.0 all-to-all-start.3
  383.0 9.2 copy.131
  392.2 96.1 %all-to-all-done.3 = bf16[8,1,2,144,2048]{4,3,2,1,0:T(8,128)(2,1)} async-done(((bf16[8,1,2,144,2048]{4,3,2,1,0:T(8,128)(2,1)}), bf16[8,1,2,144,2048]{4,3,2,1,0:T(8,128)(2,1)}, u32[]{:S(2)}, u32[]{:S(2)}) %all-to-all-start.3) | async-done | bytes 9437216 | tf_op jit(solution)/shard_map/all_to_all | solution.py:14
  488.3 9.3 copy.125
  497.5 27.3 %fusion.67 = f32[2,1152,2048]{2,1,0:T(8,128)} fusion(bf16[2,1152,2048]{2,1,0:T(8,128)(2,1)} %bitcast.192, bf16[2,2048,2048]{2,1,0:T(8,128)(2,1)} %param.28), kind=kOutput, calls=%fused_computation.174 | convolution fusion | flops 19327352832 | bytes 45088768 | tf_op jit(solution)/shard_map/erd,edf->erf/dot_general | solution.py:174
  524.9 27.5 %fusion.31 = (f32[2,1152,1024]{2,1,0:T(8,128)}, f32[2,1152,1024]{2,1,0:T(8,128)}, bf16[2,1152,1024]{2,1,0:T(8,128)(2,1)}) fusion(f32[2,1152,2048]{2,1,0:T(8,128)} %fusion.67, bf16[2,1152,2048]{2,1,0:T(8,128)(2,1)} %bitcast.194, bf16[2,1024,2048]{2,1,0:T(8,128)(2,1)} %param.29), kind=kOutput, calls=%fused_computation.95 | convolution fusion | flops 9696706560 | bytes 60293120 | tf_op jit(solution)/shard_map/erd,efd->erf/dot_general | solution.py:193
  552.4 14.6 fusion.4
  567.0 27.9 %copy.126 = bf16[1,2,1152,2048]{3,1,0,2:T(2,128)(2,1)} copy(bf16[1,2,1152,2048]{3,2,1,0:T(8,128)(2,1)S(1)} %fusion.4) | data formatting | bytes 18874368 | tf_op jit(solution)/shard_map/broadcast_in_dim | solution.py:185
  594.9 5.1 all-to-all-start.4
  600.0 27.6 %fusion.5 = bf16[1,2,1152,2048]{3,2,1,0:T(8,128)(2,1)} fusion(bf16[2,2048,2048]{2,1,0:T(8,128)(2,1)} %param.28, f32[2,1152,1024]{2,1,0:T(8,128)} %get-tuple-element.37, f32[2,1152,1024]{2,1,0:T(8,128)} %get-tuple-element.36), kind=kOutput, calls=%fused_computation.22 | convolution fusion | flops 19341508608 | bytes 45088768 | tf_op jit(solution)/shard_map/erf,edf->erd/dot_general | solution.py:203
  627.6 18.2 %copy.132 = bf16[1,2,1152,2048]{3,1,0,2:T(2,128)(2,1)} copy(bf16[1,2,1152,2048]{3,2,1,0:T(8,128)(2,1)} %fusion.5) | data formatting | bytes 18874368 | tf_op jit(solution)/shard_map/broadcast_in_dim | solution.py:215
  645.9 59.4 %all-to-all-done.4 = bf16[1,2,1152,2048]{3,1,0,2:T(2,128)(2,1)} async-done(((bf16[1,2,1152,2048]{3,1,0,2:T(2,128)(2,1)}), bf16[1,2,1152,2048]{3,1,0,2:T(2,128)(2,1)}, u32[]{:S(2)}, u32[]{:S(2)}) %all-to-all-start.4) | async-done | bytes 9437216 | tf_op jit(solution)/shard_map/all_to_all | solution.py:184
  705.3 5.0 all-to-all-start.8
  710.8 11.7 copy.127
  722.6 93.1 %all-to-all-done.8 = bf16[1,2,1152,2048]{3,1,0,2:T(2,128)(2,1)} async-done(((bf16[1,2,1152,2048]{3,1,0,2:T(2,128)(2,1)}), bf16[1,2,1152,2048]{3,1,0,2:T(2,128)(2,1)}, u32[]{:S(2)}, u32[]{:S(2)}) %all-to-all-start.8) | async-done | bytes 9437216 | tf_op jit(solution)/shard_map/all_to_all | solution.py:214
  815.6 11.8 copy.133
  827.4 21.2 %gather_fusion.1 = bf16[2048,2048]{1,0:T(8,128)(2,1)} fusion(bf16[2304,2048]{1,0:T(8,128)(2,1)} %bitcast.183, s32[2048]{0:T(1024)S(1)} %broadcast_clamp_fusion), kind=kCustom, calls=%fused_computation.1 | custom fusion | bytes 16785408 | tf_op jit(solution)/shard_map/gather | solution.py:187
  848.6 21.4 %gather_fusion.3 = bf16[2048,2048]{1,0:T(8,128)(2,1)} fusion(bf16[2304,2048]{1,0:T(8,128)(2,1)} %bitcast.184, s32[2048]{0:T(1024)S(1)} %broadcast_clamp_fusion), kind=kCustom, calls=%fused_computation.3 | custom fusion | bytes 16785408 | tf_op jit(solution)/shard_map/gather | solution.py:218
  870.0 11.4 convert_reduce_fusion
  883.6 12.9 fusion
  902.0 5.8 convolution_convert_fusion.8
  913.1 5.7 convolution_convert_fusion.4
  920.4 7.7 convolution_convert_fusion.3
  930.0 4.4 multiply_reduce_fusion
  945.4 5.7 convolution_convert_fusion.5
  955.0 5.8 convolution_convert_fusion.6
  960.9 17.9 convolution_convert_fusion.7
  978.8 10.8 reduce-scatter.11.cloned.1.call-done
  989.6 74.9 %reduce-scatter.13.cloned.1.call-done = bf16[256,2048]{1,0:T(8,128)(2,1)} async-done(((bf16[2048,2048]{1,0:T(8,128)(2,1)}), bf16[256,2048]{1,0:T(8,128)(2,1)}) %reduce-scatter.13.cloned.1.call-update) | async-done | bytes 1048592 | tf_op jit(solution)/shard_map/reduce_scatter | solution.py:283
  1064.5 75.0 %reduce-scatter.9.cloned.1.call-done = bf16[256,2048]{1,0:T(8,128)(2,1)} async-done(((bf16[2048,2048]{1,0:T(8,128)(2,1)}), bf16[256,2048]{1,0:T(8,128)(2,1)}) %reduce-scatter.9.cloned.1.call-update) | async-done | bytes 1048592 | tf_op jit(solution)/shard_map/reduce_scatter | solution.py:277
  1139.5 75.6 %reduce-scatter.7.cloned.1.call-done = bf16[256,2048]{1,0:T(8,128)(2,1)} async-done(((bf16[2048,2048]{1,0:T(8,128)(2,1)}), bf16[256,2048]{1,0:T(8,128)(2,1)}) %reduce-scatter.7.cloned.1.call-update) | async-done | bytes 1048592 | tf_op jit(solution)/shard_map/reduce_scatter | solution.py:274
  1215.2 29.3 %convolution_convert_fusion = bf16[2,2048,2048]{2,1,0:T(8,128)(2,1)} fusion(bf16[2,1152,2048]{2,1,0:T(8,128)(2,1)} %bitcast.193, f32[2,1152,1024]{2,1,0:T(8,128)} %get-tuple-element.37, f32[2,1152,1024]{2,1,0:T(8,128)} %get-tuple-element.36), kind=kOutput, calls=%fused_computation.13 | convolution fusion | flops 19345178624 | bytes 45088768 | tf_op jit(solution)/shard_map/erd,erf->edf/dot_general | solution.py:200
  1245.8 5.9 fusion.69
  1251.7 6.0 convolution_add_fusion.1
  1263.4 8.0 reduce.8
  1279.9 6.8 reduce.7
  1288.3 5.4 all-to-all-done.9
  1298.5 21.1 %all-reduce.12 = (bf16[2048]{0:T(1024)(128)(2,1)S(1)}, bf16[2048]{0:T(1024)(128)(2,1)S(1)}, bf16[128]{0:T(256)(128)(2,1)S(1)}, bf16[128]{0:T(256)(128)(2,1)S(1)}) all-reduce(bf16[2048]{0:T(1024)(128)(2,1)S(1)} %get-tuple-element.18, bf16[2048]{0:T(1024)(128)(2,1)S(1)} %get-tuple-element.16, ...), channel_id=6, replica_groups=mesh['rep'=4,'ep'=8] {'ep'}, use_global_device_ids=true, to_apply=%region_28.29.clone | all-reduce | flops 4352 | bytes 17408
  1320.0 12.4 all-reduce.14
  1343.1 19.3 %reduce-scatter.17.cloned.1.call-done = bf16[2,256,2048]{2,1,0:T(8,128)(2,1)} async-done(((bf16[2,1024,2048]{2,1,0:T(8,128)(2,1)}), bf16[2,256,2048]{2,1,0:T(8,128)(2,1)}) %reduce-scatter.17.cloned.1.call-update) | async-done | bytes 2097168 | tf_op jit(solution)/shard_map/reduce_scatter | solution.py:210
  1366.5 153.9 %all-reduce.18.cloned.1.call-done = (bf16[256,2048]{1,0:T(8,128)(2,1)}, bf16[256,2048]{1,0:T(8,128)(2,1)}, bf16[256,2048]{1,0:T(8,128)(2,1)}, bf16[256,2048]{1,0:T(8,128)(2,1)}) async-done(((bf16[256,2048]{1,0:T(8,128)(2,1)}, bf16[256,2048]{1,0:T(8,128)(2,1)}, bf16[256,2048]{1,0:T(8,128)(2,1)}, bf16[256,2048]{1,0:T(8,128)(2,1)}), (bf16[256,2048]{1,0:T(8,128)(2,1)}, bf16[256,2048]{1,0:T(8,128)(2,1)}, ...) | async-done | bytes 4194320 | tf_op jit(solution)/shard_map/psum | solution.py:300
  1529.3 273.0 %reduce-scatter.15.cloned.1.call-done = bf16[2,512,2048]{2,1,0:T(8,128)(2,1)} async-done(((bf16[2,2048,2048]{2,1,0:T(8,128)(2,1)}), bf16[2,512,2048]{2,1,0:T(8,128)(2,1)}) %reduce-scatter.15.cloned.1.call-update) | async-done | bytes 4194320 | tf_op jit(solution)/shard_map/reduce_scatter | solution.py:207
  1802.3 6.7 convert_element_type.294
  (314 shorter events, 128.4 us)
Async XLA Ops:
  7.2 26.5 %copy-start.73 = (u32[32]{0:T(128)S(1)}, u32[32]{0:T(128)}, u32[]{:S(2)}) copy-start(u32[32]{0:T(128)} %constant.91) | copy-start | bytes 388
  7.2 10.7 copy-start.53
  7.2 16.7 copy-start.74
  7.2 27.7 %copy-start.75 = (bf16[16]{0:T(256)(128)(2,1)S(1)}, bf16[16]{0:T(256)(128)(2,1)}, u32[]{:S(2)}) copy-start(bf16[16]{0:T(256)(128)(2,1)} %param.26) | copy-start | bytes 100
  7.2 28.0 %copy-start.76 = (bf16[16]{0:T(256)(128)(2,1)S(1)}, bf16[16]{0:T(256)(128)(2,1)}, u32[]{:S(2)}) copy-start(bf16[16]{0:T(256)(128)(2,1)} %param.27) | copy-start | bytes 100
  7.2 42.0 %copy-start.77 = (bf16[256]{0:T(256)(128)(2,1)S(1)}, bf16[256]{0:T(256)(128)(2,1)}, u32[]{:S(2)}) copy-start(bf16[256]{0:T(256)(128)(2,1)} %param.25) | copy-start | bytes 1540
  7.3 135.5 %all-gather.9.cloned.1.call-start = ((), (), s32[]{:S(2)}) async-start(), calls=%async_computation.17 | async-start | bytes 9437184 | tf_op jit(solution)/shard_map/all_gather | solution.py:101
  8.0 147.5 %all-gather.11.cloned.1.call-start = ((), (), s32[]{:S(2)}) async-start(), calls=%async_computation.18 | async-start | bytes 9437184 | tf_op jit(solution)/shard_map/all_gather | solution.py:102
  8.7 246.2 %all-gather.7.cloned.1.call-start = ((), (), s32[]{:S(2)}) async-start(), calls=%async_computation.16 | async-start | bytes 9437184 | tf_op jit(solution)/shard_map/all_gather | solution.py:103
  9.5 319.9 %all-gather.13.cloned.1.call-start = ((), (), s32[]{:S(2)}) async-start(), calls=%async_computation.19 | async-start | bytes 9437184 | tf_op jit(solution)/shard_map/all_gather | solution.py:104
  10.7 9.8 all-to-all-start.1
  17.9 311.5 %copy-start.59 = (f32[256]{0:T(256)}, f32[256]{0:T(256)S(1)}, u32[]{:S(2)}) copy-start(f32[256]{0:T(256)S(1)} %compare_convert_fusion) | copy-start | bytes 3076
  20.6 38.4 %all-to-all-start.2 = ((s32[8,1,256]{2,1,0:T(1,128)}), s32[8,1,256]{2,1,0:T(1,128)S(1)}, u32[]{:S(2)}, u32[]{:S(2)}) async-start(s32[8,1,256]{2,1,0:T(1,128)} %reshape.522), calls=%async_computation.2 | async-start | bytes 16384 | tf_op jit(solution)/shard_map/all_to_all | solution.py:91
  23.9 236.9 %copy-start.67 = (pred[256]{0:T(512)(128)(4,1)}, pred[256]{0:T(512)(128)(4,1)S(1)}, u32[]{:S(2)}) copy-start(pred[256]{0:T(512)(128)(4,1)S(1)} %broadcast_compare_fusion) | copy-start | bytes 772
  33.6 108.8 %copy-start.45 = (f32[8,1,256]{2,1,0:T(1,128)}, f32[8,1,256]{2,1,0:T(1,128)S(1)}, u32[]{:S(2)}) copy-start(f32[8,1,256]{2,1,0:T(1,128)S(1)} %convert_element_type.303) | copy-start | bytes 24580
  49.2 128.4 %copy-start.69 = (f32[128]{0:T(128)}, f32[128]{0:T(128)S(1)}, u32[]{:S(2)}) copy-start(f32[128]{0:T(128)S(1)} %convert_element_type.242) | copy-start | bytes 1540
  49.2 128.3 %copy-start.71 = (f32[128]{0:T(128)}, f32[128]{0:T(128)S(1)}, u32[]{:S(2)}) copy-start(f32[128]{0:T(128)S(1)} %convert_element_type.244) | copy-start | bytes 1540
  58.5 287.1 %copy-start.47 = (f32[8,1,256]{2,1,0:T(1,128)}, f32[8,1,256]{2,1,0:T(1,128)S(1)}, u32[]{:S(2)}) copy-start(f32[8,1,256]{2,1,0:T(1,128)S(1)} %convert_element_type.304) | copy-start | bytes 24580
  58.8 5.3 copy-start.43
  59.0 18.9 %all-to-all-start = ((bf16[8,32,2048]{2,1,0:T(8,128)(2,1)}), bf16[8,32,2048]{2,1,0:T(8,128)(2,1)S(1)}, u32[]{:S(2)}, u32[]{:S(2)}) async-start(bf16[8,32,2048]{2,1,0:T(8,128)(2,1)} %param.15), calls=%async_computation | async-start | bytes 2097152 | tf_op jit(solution)/shard_map/all_to_all | solution.py:84
  77.9 251.5 %copy-start.3 = (bf16[8,32,2048]{2,1,0:T(8,128)(2,1)}, bf16[8,32,2048]{2,1,0:T(8,128)(2,1)S(1)}, u32[]{:S(2)}) copy-start(bf16[8,32,2048]{2,1,0:T(8,128)(2,1)S(1)} %all-to-all-done) | copy-start | bytes 3145732
  77.9 36.1 %all-to-all-start.6 = ((bf16[8,32,2048]{2,1,0:T(8,128)(2,1)}), bf16[8,32,2048]{2,1,0:T(8,128)(2,1)}, u32[]{:S(2)}, u32[]{:S(2)}) async-start(bf16[8,32,2048]{2,1,0:T(8,128)(2,1)} %param.16), calls=%async_computation.6 | async-start | bytes 2097152 | tf_op jit(solution)/shard_map/all_to_all | solution.py:85
  82.2 16.3 copy-start.54
  114.0 28.1 %copy-start.61 = (f32[256]{0:T(256)}, f32[256]{0:T(256)S(1)}, u32[]{:S(2)}) copy-start(f32[256]{0:T(256)S(1)} %rsqrt.45) | copy-start | bytes 3076
  137.0 241.0 %all-to-all-start.7 = ((bf16[8,2,144,2048]{3,2,1,0:T(8,128)(2,1)}), bf16[8,2,144,2048]{3,2,1,0:T(8,128)(2,1)}, u32[]{:S(2)}, u32[]{:S(2)}) async-start(bf16[8,2,144,2048]{3,2,1,0:T(8,128)(2,1)} %multiply_convert_fusion), calls=%async_computation.7 | async-start | bytes 18874368 | tf_op jit(solution)/shard_map/all_to_all | solution.py:192
  142.7 31.8 %copy-start.7 = (bf16[8,32,2048]{2,1,0:T(8,128)(2,1)}, bf16[8,32,2048]{2,1,0:T(8,128)(2,1)S(1)}, u32[]{:S(2)}) copy-start(bf16[8,32,2048]{2,1,0:T(8,128)(2,1)S(1)} %fusion.28) | copy-start | bytes 3145732
  168.0 6.6 copy-start.20
  183.9 76.9 %copy-start.41 = (f32[16,256]{1,0:T(8,128)}, f32[16,256]{1,0:T(8,128)S(1)}, u32[]{:S(2)}) copy-start(f32[16,256]{1,0:T(8,128)S(1)} %log_add_fusion) | copy-start | bytes 49156
  254.9 6.9 copy-start.1
  263.0 82.6 %copy-start.21 = (bf16[16,128,256]{2,1,0:T(8,128)(2,1)}, bf16[16,128,256]{2,1,0:T(8,128)(2,1)S(1)}, u32[]{:S(2)}) copy-start(bf16[16,128,256]{2,1,0:T(8,128)(2,1)S(1)} %convolution_convert_fusion.11) | copy-start | bytes 3145732
  345.6 11.4 copy-start.63
  345.6 11.4 copy-start.56
  378.0 110.3 %all-to-all-start.3 = ((bf16[8,1,2,144,2048]{4,3,2,1,0:T(8,128)(2,1)}), bf16[8,1,2,144,2048]{4,3,2,1,0:T(8,128)(2,1)}, u32[]{:S(2)}, u32[]{:S(2)}) async-start(bf16[8,1,2,144,2048]{4,3,2,1,0:T(8,128)(2,1)} %constant_dynamic-update-slice_fusion), calls=%async_computation.3 | async-start | bytes 18874368 | tf_op jit(solution)/shard_map/all_to_all | solution.py:14
  594.9 110.4 %all-to-all-start.4 = ((bf16[1,2,1152,2048]{3,1,0,2:T(2,128)(2,1)}), bf16[1,2,1152,2048]{3,1,0,2:T(2,128)(2,1)}, u32[]{:S(2)}, u32[]{:S(2)}) async-start(bf16[1,2,1152,2048]{3,1,0,2:T(2,128)(2,1)} %copy.126), calls=%async_computation.4 | async-start | bytes 18874368 | tf_op jit(solution)/shard_map/all_to_all | solution.py:184
  645.9 64.7 %copy-start.44 = (bf16[8,8,32]{2,1,0:T(8,128)(2,1)S(1)}, bf16[8,8,32]{2,1,0:T(8,128)(2,1)}, u32[]{:S(2)}) copy-start(bf16[8,8,32]{2,1,0:T(8,128)(2,1)} %copy-done.43) | copy-start | bytes 12292
  645.9 64.8 %copy-start.60 = (f32[256]{0:T(256)S(1)}, f32[256]{0:T(256)}, u32[]{:S(2)}) copy-start(f32[256]{0:T(256)} %copy-done.59) | copy-start | bytes 3076
  645.9 64.9 %copy-start.55 = (s32[2048,1]{0,1:T(1,128)S(1)}, s32[2048,1]{0,1:T(1,128)}, u32[]{:S(2)}) copy-start(s32[2048,1]{0,1:T(1,128)} %copy-done.54) | copy-start | bytes 24580
  705.3 110.3 %all-to-all-start.8 = ((bf16[1,2,1152,2048]{3,1,0,2:T(2,128)(2,1)}), bf16[1,2,1152,2048]{3,1,0,2:T(2,128)(2,1)}, u32[]{:S(2)}, u32[]{:S(2)}) async-start(bf16[1,2,1152,2048]{3,1,0,2:T(2,128)(2,1)} %copy.132), calls=%async_computation.8 | async-start | bytes 18874368 | tf_op jit(solution)/shard_map/all_to_all | solution.py:214
  710.3 279.3 %reduce-scatter.11.cloned.1.call-start = ((), (), s32[]{:S(2)}) async-start(), calls=%async_computation.22 | async-start | bytes 9437184 | tf_op jit(solution)/shard_map/reduce_scatter | solution.py:280
  870.0 11.5 copy-start.6
  870.0 11.4 copy-start.48
  870.0 11.4 copy-start.57
  902.0 6.3 copy-start.42
  902.0 6.3 copy-start.68
  907.8 5.3 copy-start.8
  908.3 10.5 copy-start.23
  918.8 145.7 %reduce-scatter.13.cloned.1.call-start = ((), (), s32[]{:S(2)}) async-start(), calls=%async_computation.23 | async-start | bytes 9437184 | tf_op jit(solution)/shard_map/reduce_scatter | solution.py:283
  928.1 211.4 %reduce-scatter.9.cloned.1.call-start = ((), (), s32[]{:S(2)}) async-start(), calls=%async_computation.21 | async-start | bytes 9437184 | tf_op jit(solution)/shard_map/reduce_scatter | solution.py:277
  951.1 264.0 %reduce-scatter.7.cloned.1.call-start = ((), (), s32[]{:S(2)}) async-start(), calls=%async_computation.20 | async-start | bytes 9437184 | tf_op jit(solution)/shard_map/reduce_scatter | solution.py:274
  960.8 401.6 %reduce-scatter.17.cloned.1.call-start = ((), (), s32[]{:S(2)}) async-start(), calls=%async_computation.25 | async-start | bytes 10485760 | tf_op jit(solution)/shard_map/reduce_scatter | solution.py:210
  978.8 541.6 %all-reduce.18.cloned.1.call-start = ((), (), s32[]{:S(2)}) async-start(), calls=%async_computation.26 | async-start | bytes 8388608 | tf_op jit(solution)/shard_map/psum | solution.py:300
  1215.1 587.1 %reduce-scatter.15.cloned.1.call-start = ((), (), s32[]{:S(2)}) async-start(), calls=%async_computation.24 | async-start | bytes 20971520 | tf_op jit(solution)/shard_map/reduce_scatter | solution.py:207
  1245.8 5.9 copy-start.26
  1245.8 12.0 slice-start
  1251.7 6.1 copy-start.4
  1251.7 6.1 copy-start.32
  1251.7 6.1 copy-start.46
  1251.7 6.1 copy-start.62
  1251.7 6.1 slice-start.1
  1262.9 15.4 copy-start.22
  1274.0 19.6 %all-to-all-start.9 = ((bf16[8,2,32768]{2,1,0:T(2,128)(2,1)}), bf16[8,2,32768]{2,1,0:T(2,128)(2,1)}, u32[]{:S(2)}, u32[]{:S(2)}) async-start(bf16[8,2,32768]{2,1,0:T(2,128)(2,1)} %reshape.528), calls=%async_computation.9 | async-start | bytes 2097152 | tf_op jit(solution)/shard_map/all_to_all | solution.py:271
  1293.7 46.8 %all-to-all-start.5 = ((bf16[8,2,32768]{2,1,0:T(2,128)(2,1)}), bf16[8,2,32768]{2,1,0:T(2,128)(2,1)S(1)}, u32[]{:S(2)}, u32[]{:S(2)}) async-start(bf16[8,2,32768]{2,1,0:T(2,128)(2,1)} %reshape.526), calls=%async_computation.5 | async-start | bytes 2097152 | tf_op jit(solution)/shard_map/all_to_all | solution.py:268
  1520.4 5.7 copy-start.30
  1520.4 7.3 copy-start.29
  (37 other events, 71.9 us)
Sparse Core Ops, SparseCore 0:
  9.9 57.3 all-gather.8
  69.2 65.4 all-gather.10
  136.5 118.3 all-gather.6
  256.7 72.6 all-gather.12
  919.0 70.6 reduce-scatter.10
  993.0 71.5 reduce-scatter.12
  1068.0 71.5 reduce-scatter.8
  1143.6 71.5 reduce-scatter.6
  1217.5 144.8 reduce-scatter.16
  1364.8 155.5 all-reduce.17
  1522.8 279.4 reduce-scatter.14
